TPU v7x, 512 devices: a whole 4x8x8 slice. The times are simulated.
512 devices in a mesh: pool: 16 (over z, y_hi), fft: 32 (over x, y_lo, core).
Axes of the slice: x: 4, y: 8 (y_hi: 2, y_lo: 4; y = y_hi * 4 + y_lo), z: 8, core: 2. Of those that a mesh axis runs over, the one named last changes fastest.
Arguments:
- orbitals: bfloat16 [16, 2, 1, 160, 25600], P('pool', None, None, 'fft'), may hold values from -6 to 6
- stick_map: int32 [16000], replicated, may hold values from -1 to 25599, as said below
- kpoint_grid: int32 [16, 3], replicated, may hold values from 0 to 3, as said below
Outputs:
- exchange_action: bfloat16 [16, 2, 1, 160, 25600], P('pool', None, None, 'fft')
Inputs may be any that keep to these rules, and one draw needn't show every extreme that they name: `stick_map`: entries other than -1 are distinct columns. Slots come in blocks of 500 per index of fft; in each block at least half of the slots are live, and in every draw some block has all 500 live. `kpoint_grid`: rows are distinct.
All inputs are finite; a program needn't handle non-finite values.
Results may differ from a plain program's by a relative error of at most 0.011.
Values may be sent and summed in bfloat16 or wider, within the bound.
A program may use at most 64 MiB of HBM per device.

v0:
```python
import math
import jax
import jax.numpy as jnp
from jax import lax
from jax.sharding import PartitionSpec as P

NG = 160
KMESH = 4
SPACING_BOHR = 0.1875
SCREENING = 0.106


def shifted(value, axis, steps):
    count = lax.axis_size(axis)
    pairs = [(source, (source + steps) % count) for source in range(count)]
    return lax.ppermute(value, axis, pairs)


def dft_table(grid_size, orientation):
    positions = jnp.arange(grid_size, dtype=jnp.int32)
    product = positions[:, None] * positions[None, :] % grid_size
    angle = product.astype(jnp.float32) * (2.0 * math.pi / grid_size)
    cosine = jnp.cos(angle)
    sine = orientation * jnp.sin(angle)
    upper = jnp.stack([cosine, sine], axis=1)
    lower = jnp.stack([-sine, cosine], axis=1)
    return jnp.stack([upper, lower], axis=0).astype(jnp.bfloat16)


def signed(frequency, grid_size):
    return jnp.where(frequency >= grid_size // 2, frequency - grid_size, frequency)


def kernel_table(columns, shift_q, grid_size):
    live_slot = columns >= 0
    column_ids = jnp.where(live_slot, columns, 0)
    freq_x = signed(column_ids % grid_size, grid_size)
    freq_y = signed(column_ids // grid_size, grid_size)
    freq_z = signed(jnp.arange(grid_size, dtype=jnp.int32), grid_size)
    radius = grid_size // 2
    inside = (freq_x * freq_x + freq_y * freq_y)[None, :] + (freq_z * freq_z)[
        :, None
    ] <= radius * radius
    inside = jnp.logical_and(inside, live_slot[None, :])
    wave_x = freq_x.astype(jnp.float32) + shift_q[0]
    wave_y = freq_y.astype(jnp.float32) + shift_q[1]
    wave_z = freq_z.astype(jnp.float32) + shift_q[2]
    square = (wave_z * wave_z)[:, None] + (wave_x * wave_x + wave_y * wave_y)[None, :]
    cell = SPACING_BOHR * grid_size
    exponent = math.pi * math.pi * square / (cell * cell * SCREENING * SCREENING)
    weights = cell * cell / math.pi * -jnp.expm1(-exponent) / square / float(grid_size) ** 3
    return jnp.where(inside, weights, 0.0)


def momentum(kpoint_grid, pool_rank, pool_count):
    pool_rows = jnp.arange(pool_count, dtype=jnp.int32)
    earlier = (pool_rank + pool_count - 1) % pool_count
    current = jnp.sum(jnp.where((pool_rows == pool_rank)[:, None], kpoint_grid, 0), axis=0)
    previous = jnp.sum(jnp.where((pool_rows == earlier)[:, None], kpoint_grid, 0), axis=0)
    return (current - previous).astype(jnp.float32) / KMESH


def pair_density(own_bands, received):
    band_count = own_bands.shape[1]
    real_own = own_bands[0].astype(jnp.float32)[:, None]
    imag_own = own_bands[1].astype(jnp.float32)[:, None]
    real_recv = received[0].astype(jnp.float32)[None]
    imag_recv = received[1].astype(jnp.float32)[None]
    real_part = real_recv * real_own + imag_recv * imag_own
    imag_part = real_recv * imag_own - imag_recv * real_own
    stacked = jnp.stack([real_part, imag_part], axis=2)
    return stacked.reshape((band_count * band_count, 2) + own_bands.shape[2:]).astype(jnp.bfloat16)


def action_of(received, field):
    band_count = received.shape[1]
    field = field.reshape((band_count, band_count) + field.shape[1:])
    real_recv = received[0].astype(jnp.float32)[None]
    imag_recv = received[1].astype(jnp.float32)[None]
    real_field = field[:, :, 0]
    imag_field = field[:, :, 1]
    real_part = -jnp.sum(real_recv * real_field - imag_recv * imag_field, axis=1)
    imag_part = -jnp.sum(real_recv * imag_field + imag_recv * real_field, axis=1)
    return jnp.stack([real_part, imag_part], axis=0).astype(jnp.bfloat16)


def apply_table(data, table, form):
    return jnp.einsum(form, data, table, preferred_element_type=jnp.float32)


def column_pass(picked, weights, forward, backward):
    spectrum = apply_table(picked, forward, "pczs,czdk->pdks")
    scaled = (spectrum * weights).astype(jnp.bfloat16)
    return apply_table(scaled, backward, "pczs,czdk->pdks").astype(jnp.bfloat16)


def local(orbitals, stick_map, kpoint_grid):
    grid_size = NG
    moved = shifted(orbitals, "pool", 1)
    own_bands = orbitals[0].reshape(orbitals.shape[1:4] + (grid_size, grid_size))
    received = moved[0].reshape(orbitals.shape[1:4] + (grid_size, grid_size))
    fft_count = lax.axis_size("fft")
    fft_rank = lax.axis_index("fft")
    pool_count = lax.axis_size("pool")
    pool_rank = lax.axis_index("pool")
    shift_q = momentum(kpoint_grid, pool_rank, pool_count)
    forward = dft_table(grid_size, -1.0)
    backward = dft_table(grid_size, 1.0)
    column_share = grid_size * grid_size // fft_count
    share_ids = fft_rank * column_share + jnp.arange(column_share, dtype=jnp.int32)
    own_rows = fft_rank * (grid_size // fft_count) + jnp.arange(
        grid_size // fft_count, dtype=jnp.int32
    )
    row_hit = (stick_map[None, :] // grid_size == own_rows[:, None]) & (stick_map >= 0)[None, :]
    every_column = jnp.arange(grid_size, dtype=jnp.int32)
    column_hit = stick_map[None, :] % grid_size == every_column[:, None]
    counts = jnp.einsum(
        "rs,cs->rc",
        row_hit.astype(jnp.bfloat16),
        column_hit.astype(jnp.bfloat16),
        preferred_element_type=jnp.float32,
    )
    own_present = counts.reshape(column_share) > 0.5
    weights = kernel_table(jnp.where(own_present, share_ids, -1), shift_q, grid_size)

    def potential(pair_block):
        along_x = apply_table(pair_block, forward, "pczyx,cxek->pezyk").astype(jnp.bfloat16)
        along_y = apply_table(along_x, forward, "pczyx,cyek->pezkx").astype(jnp.bfloat16)
        piece_block = lax.all_to_all(along_y, "fft", split_axis=3, concat_axis=2, tiled=True)
        flat_piece = piece_block.reshape(piece_block.shape[:3] + (column_share,))
        scaled_back = column_pass(flat_piece, weights, forward, backward).reshape(piece_block.shape)
        spectrum = lax.all_to_all(scaled_back, "fft", split_axis=2, concat_axis=3, tiled=True)
        back_y = apply_table(spectrum, backward, "pczkx,ckey->pezyx").astype(jnp.bfloat16)
        return apply_table(back_y, backward, "pczyk,ckex->pezyx")

    density = pair_density(own_bands, received)
    field = lax.map(lambda single_pair: potential(single_pair[None])[0], density)
    result = action_of(received, field)
    return result.reshape((1,) + result.shape[:3] + (grid_size * grid_size,))


def solution(mesh):
    return jax.shard_map(
        local,
        mesh=mesh,
        in_specs=(P("pool", None, None, "fft", None), P(), P()),
        out_specs=P("pool", None, None, "fft", None),
        check_vma=False,
    )
```

profile of v0, /device:TPU:1, one launch (start us, length us, event | category | flops | bytes accessed | tf_op | source)
XLA Modules:
  0.0 118.0 jit_solution(2469198560050355938)
XLA Ops:
  0.0 8.3 %collective-permute-start = (bf16[1,2,1,5,25600]{4,1,3,2,0:T(2,128)(2,1)}, bf16[1,2,1,5,25600]{4,1,3,2,0:T(2,128)(2,1)S(1)}, u32[]{:S(2)}, u32[]{:S(2)}) collective-permute-start(bf16[1,2,1,5,25600]{4,1,3,2,0:T(2,128)(2,1)} %param.3), channel_id=1, source_target_pairs={{0,32},{32,64},{64,96},{96,128},{128,160},{160,192},{192,224},{224... | collective-permute-start | bytes 1536008 | tf_op jit(solution)/shard_map/ppermute | solution.py:16
  8.3 0.9 add_select_fusion.2
  9.2 0.9 broadcast_compare_fusion
  10.1 0.8 select_reduce_fusion
  10.9 0.7 fusion.74
  11.6 1.9 %fusion.9 = pred[5,160]{1,0:T(8,128)(4,1)S(1)} fusion(s32[16000]{0:T(1024)S(1)} %get-tuple-element.36, s32[16000]{0:T(1024)S(1)} %get-tuple-element.35, s32[5]{0:T(128)S(1)} %iota_add_fusion, pred[16000]{0:T(1024)(128)(4,1)S(1)} %broadcast_compare_fusion), kind=kOutput, calls=%fused_computation.16 | convolution fusion | flops 28320800 | bytes 144820 | tf_op jit(solution)/shard_map/rs,cs->rc/dot_general | solution.py:117
  13.6 0.7 fusion.59
  14.3 0.7 cosine_convert_fusion
  15.0 0.7 negate_convert_fusion.2
  15.7 16.1 %collective-permute-done = bf16[1,2,1,5,25600]{4,1,3,2,0:T(2,128)(2,1)S(1)} collective-permute-done((bf16[1,2,1,5,25600]{4,1,3,2,0:T(2,128)(2,1)}, bf16[1,2,1,5,25600]{4,1,3,2,0:T(2,128)(2,1)S(1)}, u32[]{:S(2)}, u32[]{:S(2)}) %collective-permute-start) | collective-permute-done | bytes 512032 | tf_op jit(solution)/shard_map/ppermute | solution.py:16
  31.8 4.2 %fusion.35 = (bf16[5,25600]{1,0:T(8,128)(2,1)S(1)}, bf16[5,25600]{1,0:T(8,128)(2,1)S(1)}) fusion(bf16[1,2,1,5,25600]{4,1,3,2,0:T(2,128)(2,1)S(1)} %copy-done, bf16[1,2,1,5,25600]{4,1,3,2,0:T(2,128)(2,1)S(1)} %collective-permute-done), kind=kLoop, calls=%fused_computation.53 | loop fusion | flops 1536000 | bytes 1536000 | tf_op jit(solution)/shard_map/convert.5
  36.5 0.5 add.242
  37.1 1.0 fusion.7
  38.1 1.8 %copy.79 = bf16[1,2,5,160,160]{4,1,2,0,3:T(2,128)(2,1)} copy(bf16[1,2,5,160,160]{4,3,2,1,0:T(8,128)(2,1)S(1)} %fusion.7) | data formatting | bytes 1024000 | tf_op jit(solution)/shard_map/while/body/eval_jaxpr/convert_element_type | solution.py:128
  39.9 13.5 %all-to-all-start = ((bf16[1,2,5,160,160]{4,1,2,0,3:T(2,128)(2,1)}), bf16[1,2,5,160,160]{4,1,2,0,3:T(2,128)(2,1)S(1)}, u32[]{:S(2)}, u32[]{:S(2)}) async-start(bf16[1,2,5,160,160]{4,1,2,0,3:T(2,128)(2,1)} %copy.79), calls=%async_computation | async-start | bytes 1638400 | tf_op jit(solution)/shard_map/while/body/eval_jaxpr/all_to_all | solution.py:129
  53.3 0.6 add_multiply_fusion.1
  53.9 1.3 %multiply_add_fusion = f32[800]{0:T(1024)S(1)} fusion(f32[]{:T(128)} %bitcast.30, f32[]{:T(128)} %bitcast.29, pred[800]{0:T(1024)(128)(4,1)S(1)} %gt.21, s32[]{:T(128)S(6)} %mul.330), kind=kLoop, calls=%fused_computation.98 | loop fusion | flops 23200 | bytes 4012 | tf_op jit(solution)/shard_map/add | solution.py:48
  55.2 0.5 fusion.21
  55.8 20.6 %all-to-all-done = bf16[1,2,5,160,160]{4,1,2,0,3:T(2,128)(2,1)S(1)} async-done(((bf16[1,2,5,160,160]{4,1,2,0,3:T(2,128)(2,1)}), bf16[1,2,5,160,160]{4,1,2,0,3:T(2,128)(2,1)S(1)}, u32[]{:S(2)}, u32[]{:S(2)}) %all-to-all-start) | async-done | bytes 512032 | tf_op jit(solution)/shard_map/while/body/eval_jaxpr/all_to_all | solution.py:129
  76.3 0.6 copy.80
  77.1 1.1 reshape.574
  78.2 1.8 %fusion.4 = bf16[2,160,800]{2,1,0:T(8,128)(2,1)S(1)} fusion(bf16[2,160,800,1]{2,1,0,3:T(8,128)(2,1)S(1)} %reshape.574, f32[160,800]{1,0:T(8,128)S(1)} %fusion.21, bf16[1,160,2,160]{1,3,0,2:T(8,128)(2,1)S(1)} %get-tuple-element.32, bf16[1,160,2,160]{1,3,0,2:T(8,128)(2,1)} %copy-done.1, bf16[1,160,2,160]{1,3,2,0:T(8,128)(2,1)S(1)} %get-tuple-element.34, ...), kind=kOutput, calls=%fused_computation.11 | convolution fusion | flops 328652800 | bytes 1945600 | tf_op jit(solution)/shard_map/while/body/eval_jaxpr/pczs,czdk->pdks/dot_general | solution.py:88
  80.3 1.7 %copy.83 = bf16[1,2,160,5,160]{4,1,3,0,2:T(2,128)(2,1)S(1)} copy(bf16[1,2,160,5,160]{2,4,3,1,0:T(8,128)(2,1)S(1)} %bitcast.188) | data formatting | bytes 1024000 | tf_op jit(solution)/shard_map/while/body/eval_jaxpr/reshape | solution.py:131
  82.0 26.6 %all_to_all.38 = bf16[1,2,160,5,160]{4,1,3,0,2:T(2,128)(2,1)S(1)} all-to-all(bf16[1,2,160,5,160]{4,1,3,0,2:T(2,128)(2,1)S(1)} %copy.83), channel_id=1, replica_groups=mesh['pool'=16,'fft'=32] {'fft'}, dimensions={2} | all-to-all | bytes 1024000 | tf_op jit(solution)/shard_map/while/body/eval_jaxpr/all_to_all | solution.py:132
  108.6 0.6 copy.84
  109.2 0.6 fusion.6
  109.8 0.6 convolution_bitcast_fusion
  110.9 0.9 squeeze.29
  112.3 0.9 squeeze.28
  113.2 1.8 %negate_convert_fusion.1 = (bf16[1,1,1,5,25600]{4,2,3,1,0:T(2,128)(2,1)S(1)}, bf16[1,1,1,5,25600]{4,2,3,1,0:T(2,128)(2,1)S(1)}) fusion(f32[1,1,1,5,25600]{4,2,3,1,0:T(1,128)S(1)} %squeeze.29, f32[1,1,1,5,25600]{4,2,3,1,0:T(1,128)S(1)} %squeeze.28, bf16[1,2,1,5,25600]{4,1,3,2,0:T(2,128)(2,1)S(1)} %collective-permute-done), kind=kLoop, calls=%fused_computation.51 | loop fusion | flops 1536000 | bytes 2048000 | tf_op jit(solution)/shard_map/convert
  115.0 1.7 %pad_maximum_fusion = bf16[1,2,1,5,25600]{4,2,3,1,0:T(2,128)(2,1)S(1)} fusion(bf16[1,1,1,5,25600]{4,2,3,1,0:T(2,128)(2,1)S(1)} %get-tuple-element.30, bf16[1,1,1,5,25600]{4,2,3,1,0:T(2,128)(2,1)S(1)} %get-tuple-element.29), kind=kLoop, calls=%fused_computation.17 | loop fusion | flops 256000 | bytes 1024000 | tf_op jit(solution)/shard_map/stack | solution.py:84
  116.7 1.3 %copy.91 = bf16[1,2,1,5,25600]{4,1,3,2,0:T(2,128)(2,1)} copy(bf16[1,2,1,5,25600]{4,2,3,1,0:T(2,128)(2,1)S(1)} %pad_maximum_fusion) | data formatting | bytes 1024000 | tf_op jit(solution)/shard_map/stack | solution.py:84
  (18 shorter events, 2.2 us)
Async XLA Ops:
  0.0 31.8 %collective-permute-start = (bf16[1,2,1,5,25600]{4,1,3,2,0:T(2,128)(2,1)}, bf16[1,2,1,5,25600]{4,1,3,2,0:T(2,128)(2,1)S(1)}, u32[]{:S(2)}, u32[]{:S(2)}) collective-permute-start(bf16[1,2,1,5,25600]{4,1,3,2,0:T(2,128)(2,1)} %param.3), channel_id=1, source_target_pairs={{0,32},{32,64},{64,96},{96,128},{128,160},{160,192},{192,224},{224... | collective-permute-start | bytes 1536008 | tf_op jit(solution)/shard_map/ppermute | solution.py:16
  11.6 20.2 %copy-start = (bf16[1,2,1,5,25600]{4,1,3,2,0:T(2,128)(2,1)S(1)}, bf16[1,2,1,5,25600]{4,1,3,2,0:T(2,128)(2,1)}, u32[]{:S(2)}) copy-start(bf16[1,2,1,5,25600]{4,1,3,2,0:T(2,128)(2,1)} %param.3) | copy-start | bytes 1536004
  15.7 24.1 %copy-start.1 = (bf16[1,160,2,160]{1,3,0,2:T(8,128)(2,1)}, bf16[1,160,2,160]{1,3,0,2:T(8,128)(2,1)S(1)}, u32[]{:S(2)}) copy-start(bf16[1,160,2,160]{1,3,0,2:T(8,128)(2,1)S(1)} %get-tuple-element.33) | copy-start | bytes 307204
  39.9 36.5 %all-to-all-start = ((bf16[1,2,5,160,160]{4,1,2,0,3:T(2,128)(2,1)}), bf16[1,2,5,160,160]{4,1,2,0,3:T(2,128)(2,1)S(1)}, u32[]{:S(2)}, u32[]{:S(2)}) async-start(bf16[1,2,5,160,160]{4,1,2,0,3:T(2,128)(2,1)} %copy.79), calls=%async_computation | async-start | bytes 1638400 | tf_op jit(solution)/shard_map/while/body/eval_jaxpr/all_to_all | solution.py:129
where the time goes:
time: 118 us
  waiting for transfers between devices  36.6 us (31%)
  blocking collectives  26.6 us (23%)
  starting transfers between devices  21.7 us (18%)
  other arithmetic  14.8 us (13%)
  local copies, waits for them, and re-layouts  12.1 us (10%)
  matrix products  5.98 us (5%)
    all_to_all x1, blocking collectives, potential(): lax.all_to_all(scaled_back, 'fft', split_axis=2, concat_axis=3, tiled=True)  26.6 us
    all_to_all x1, waiting for transfers between devices, potential(): lax.all_to_all(along_y, 'fft', split_axis=3, concat_axis=2, tiled=True)  20.6 us
    ppermute x1, waiting for transfers between devices, shifted(): return lax.ppermute(value, axis, pairs)  16.1 us
    all_to_all x1, starting transfers between devices, potential(): lax.all_to_all(along_y, 'fft', split_axis=3, concat_axis=2, tiled=True)  13.5 us
    ppermute x1, starting transfers between devices, shifted(): return lax.ppermute(value, axis, pairs)  8.26 us
    another operation x5, other arithmetic  7.94 us
    dot_general x4, matrix products, apply_table(): return jnp.einsum(form, data, table, preferred_element_type=jnp.float32)  4.06 us
  transfers between devices with their start and end apart: 2, of which 2 were waited for; matrix products, arithmetic and copies ran while one was open for 8% of the time, Pallas kernels for 0%

commit v1 on v0

--- a/solution.py
+++ b/solution.py
@@ -129,7 +129,12 @@
         piece_block = lax.all_to_all(along_y, "fft", split_axis=3, concat_axis=2, tiled=True)
         flat_piece = piece_block.reshape(piece_block.shape[:3] + (column_share,))
         scaled_back = column_pass(flat_piece, weights, forward, backward).reshape(piece_block.shape)
-        spectrum = lax.all_to_all(scaled_back, "fft", split_axis=2, concat_axis=3, tiled=True)
+        spectrum = jnp.concatenate(
+            lax.all_to_all(
+                jnp.stack(jnp.split(scaled_back, lax.axis_size("fft"), axis=2)), "fft", 0, 0
+            ),
+            axis=3,
+        )
         back_y = apply_table(spectrum, backward, "pczkx,ckey->pezyx").astype(jnp.bfloat16)
         return apply_table(back_y, backward, "pczyk,ckex->pezyx")
 

time: 118 us -> 161 us (1.36)
  local copies, waits for them, and re-layouts: 12.1 us -> 53 us
    unnamed x4 -> x35, local copies, waits for them, and re-layouts: 0.01 us -> 29.1 us
    another operation x1 -> x3, local copies, waits for them, and re-layouts: 1.07 us -> 14.6 us  [the longest x2 13.5 us: potential(): jnp.stack(jnp.split(scaled_back, lax.axis_size('fft'), axis=2))]
  transfers between devices with their start and end apart: 2 -> 2, of which waited for: 2 -> 2; matrix products, arithmetic and copies ran while one was open for 8% -> 6% of each run, Pallas kernels for 0% -> 0%
where the time goes in v1:
time: 161 us; the launch traced here: 160 us
  local copies, waits for them, and re-layouts  53 us (33%)
  waiting for transfers between devices  36.5 us (23%)
  blocking collectives  26.6 us (17%)
  starting transfers between devices  21.7 us (13%)
  other arithmetic  16 us (10%)
  matrix products  6.05 us (4%)
    unnamed x35, local copies, waits for them, and re-layouts  29.1 us
    all_to_all x1, blocking collectives, potential(): lax.all_to_all(jnp.stack(jnp.split(scaled_back, lax.axis_size('fft'), axi...  26.6 us
    all_to_all x1, waiting for transfers between devices, potential(): lax.all_to_all(along_y, 'fft', split_axis=3, concat_axis=2, tiled=True)  20.5 us
    ppermute x1, waiting for transfers between devices, shifted(): return lax.ppermute(value, axis, pairs)  16 us
    another operation x2, local copies, waits for them, and re-layouts, potential(): jnp.stack(jnp.split(scaled_back, lax.axis_size('fft'), axis=2))  13.5 us
    all_to_all x1, starting transfers between devices, potential(): lax.all_to_all(along_y, 'fft', split_axis=3, concat_axis=2, tiled=True)  13.5 us
    another operation x5, other arithmetic  9.1 us
    ppermute x1, starting transfers between devices, shifted(): return lax.ppermute(value, axis, pairs)  8.26 us
  transfers between devices with their start and end apart: 2, of which 2 were waited for; matrix products, arithmetic and copies ran while one was open for 6% of the time, Pallas kernels for 0%

profile of v1, /device:TPU:1, one launch (start us, length us, event | category | flops | bytes accessed | tf_op | source)
XLA Modules:
  0.0 160.2 jit_solution(4685730104756746464)
XLA Ops:
  0.0 8.3 %collective-permute-start = (bf16[1,2,1,5,25600]{4,1,3,2,0:T(2,128)(2,1)}, bf16[1,2,1,5,25600]{4,1,3,2,0:T(2,128)(2,1)S(1)}, u32[]{:S(2)}, u32[]{:S(2)}) collective-permute-start(bf16[1,2,1,5,25600]{4,1,3,2,0:T(2,128)(2,1)} %param.3), channel_id=1, source_target_pairs={{0,32},{32,64},{64,96},{96,128},{128,160},{160,192},{192,224},{224... | collective-permute-start | bytes 1536008 | tf_op jit(solution)/shard_map/ppermute | solution.py:16
  11.6 1.9 %fusion.9 = pred[5,160]{1,0:T(8,128)(4,1)S(1)} fusion(s32[16000]{0:T(1024)S(1)} %get-tuple-element.36, s32[16000]{0:T(1024)S(1)} %get-tuple-element.35, s32[5]{0:T(128)S(1)} %iota_add_fusion, pred[16000]{0:T(1024)(128)(4,1)S(1)} %broadcast_compare_fusion), kind=kOutput, calls=%fused_computation.16 | convolution fusion | flops 28320800 | bytes 144820 | tf_op jit(solution)/shard_map/rs,cs->rc/dot_general | solution.py:117
  15.8 16.0 %collective-permute-done = bf16[1,2,1,5,25600]{4,1,3,2,0:T(2,128)(2,1)S(1)} collective-permute-done((bf16[1,2,1,5,25600]{4,1,3,2,0:T(2,128)(2,1)}, bf16[1,2,1,5,25600]{4,1,3,2,0:T(2,128)(2,1)S(1)}, u32[]{:S(2)}, u32[]{:S(2)}) %collective-permute-start) | collective-permute-done | bytes 512032 | tf_op jit(solution)/shard_map/ppermute | solution.py:16
  31.8 5.3 %fusion.35 = (bf16[5,25600]{1,0:T(8,128)(2,1)S(1)}, bf16[5,25600]{1,0:T(8,128)(2,1)S(1)}) fusion(bf16[1,2,1,5,25600]{4,1,3,2,0:T(2,128)(2,1)} %param.3, bf16[1,2,1,5,25600]{4,1,3,2,0:T(2,128)(2,1)S(1)} %collective-permute-done), kind=kLoop, calls=%fused_computation.53 | loop fusion | flops 1536000 | bytes 1536000 | tf_op jit(solution)/shard_map/convert.5
  38.2 1.0 fusion.7
  39.3 1.8 %copy.144 = bf16[1,2,5,160,160]{4,1,2,0,3:T(2,128)(2,1)} copy(bf16[1,2,5,160,160]{4,3,2,1,0:T(8,128)(2,1)S(1)} %fusion.7) | data formatting | bytes 1024000 | tf_op jit(solution)/shard_map/while/body/eval_jaxpr/convert_element_type | solution.py:128
  41.0 13.5 %all-to-all-start = ((bf16[1,2,5,160,160]{4,1,2,0,3:T(2,128)(2,1)}), bf16[1,2,5,160,160]{4,1,2,0,3:T(2,128)(2,1)S(1)}, u32[]{:S(2)}, u32[]{:S(2)}) async-start(bf16[1,2,5,160,160]{4,1,2,0,3:T(2,128)(2,1)} %copy.144), calls=%async_computation | async-start | bytes 1638400 | tf_op jit(solution)/shard_map/while/body/eval_jaxpr/all_to_all | solution.py:129
  55.2 1.2 multiply_add_fusion
  57.0 20.5 %all-to-all-done = bf16[1,2,5,160,160]{4,1,2,0,3:T(2,128)(2,1)S(1)} async-done(((bf16[1,2,5,160,160]{4,1,2,0,3:T(2,128)(2,1)}), bf16[1,2,5,160,160]{4,1,2,0,3:T(2,128)(2,1)S(1)}, u32[]{:S(2)}, u32[]{:S(2)}) %all-to-all-start) | async-done | bytes 512032 | tf_op jit(solution)/shard_map/while/body/eval_jaxpr/all_to_all | solution.py:129
  78.3 1.1 reshape.581
  79.4 1.9 %fusion.4 = bf16[2,160,800]{2,1,0:T(8,128)(2,1)S(1)} fusion(bf16[2,160,800,1]{2,1,0,3:T(8,128)(2,1)S(1)} %reshape.581, f32[160,800]{1,0:T(8,128)S(1)} %fusion.21, bf16[1,160,2,160]{1,3,0,2:T(8,128)(2,1)} %copy-done, bf16[1,160,2,160]{1,3,0,2:T(8,128)(2,1)} %copy-done.1, bf16[1,160,2,160]{1,3,2,0:T(8,128)(2,1)S(1)} %get-tuple-element.34, ...), kind=kOutput, calls=%fused_computation.11 | convolution fusion | flops 328652800 | bytes 1945600 | tf_op jit(solution)/shard_map/while/body/eval_jaxpr/pczs,czdk->pdks/dot_general | solution.py:88
  82.4 0.9 fusion.68
  83.3 0.9 fusion.67
  88.0 0.9 fusion.62
  89.9 0.9 fusion.60
  93.6 1.0 fusion.56
  95.5 0.9 fusion.54
  97.4 0.9 fusion.52
  100.2 1.0 fusion.49
  101.2 1.0 fusion.48
  102.2 1.0 fusion.47
  105.0 0.9 fusion.44
  105.9 1.0 fusion.43
  106.9 1.0 fusion.42
  110.7 1.0 fusion.38
  111.6 12.6 %copy.148 = bf16[32,1,2,5,5,160]{5,2,4,3,1,0:T(2,128)(2,1)S(1)} copy(bf16[32,1,2,5,5,160]{3,5,4,2,1,0:T(8,128)(2,1)} %fusion.38) | data formatting | bytes 1024000 | tf_op jit(solution)/shard_map/while/body/eval_jaxpr/stack | solution.py:134
  124.2 26.6 %all_to_all.25 = bf16[32,1,2,5,5,160]{5,2,4,3,1,0:T(2,128)(2,1)S(1)} all-to-all(bf16[32,1,2,5,5,160]{5,2,4,3,1,0:T(2,128)(2,1)S(1)} %copy.148), channel_id=1, replica_groups=mesh['pool'=16,'fft'=32] {'fft'}, dimensions={0} | all-to-all | bytes 1024000 | tf_op jit(solution)/shard_map/while/body/eval_jaxpr/all_to_all | solution.py:133
  153.1 0.9 squeeze.29
  154.4 0.9 squeeze.28
  155.4 1.8 %negate_convert_fusion.1 = (bf16[1,1,1,5,25600]{4,2,3,1,0:T(2,128)(2,1)S(1)}, bf16[1,1,1,5,25600]{4,2,3,1,0:T(2,128)(2,1)S(1)}) fusion(f32[1,1,1,5,25600]{4,2,3,1,0:T(1,128)S(1)} %squeeze.29, f32[1,1,1,5,25600]{4,2,3,1,0:T(1,128)S(1)} %squeeze.28, bf16[1,2,1,5,25600]{4,1,3,2,0:T(2,128)(2,1)S(1)} %collective-permute-done), kind=kLoop, calls=%fused_computation.51 | loop fusion | flops 1536000 | bytes 2048000 | tf_op jit(solution)/shard_map/convert
  157.2 1.7 %pad_maximum_fusion = bf16[1,2,1,5,25600]{4,2,3,1,0:T(2,128)(2,1)S(1)} fusion(bf16[1,1,1,5,25600]{4,2,3,1,0:T(2,128)(2,1)S(1)} %get-tuple-element.30, bf16[1,1,1,5,25600]{4,2,3,1,0:T(2,128)(2,1)S(1)} %get-tuple-element.29), kind=kLoop, calls=%fused_computation.17 | loop fusion | flops 256000 | bytes 1024000 | tf_op jit(solution)/shard_map/stack | solution.py:84
  158.9 1.3 copy.156
  (50 shorter events, 28.2 us)
Async XLA Ops:
  0.0 31.8 %collective-permute-start = (bf16[1,2,1,5,25600]{4,1,3,2,0:T(2,128)(2,1)}, bf16[1,2,1,5,25600]{4,1,3,2,0:T(2,128)(2,1)S(1)}, u32[]{:S(2)}, u32[]{:S(2)}) collective-permute-start(bf16[1,2,1,5,25600]{4,1,3,2,0:T(2,128)(2,1)} %param.3), channel_id=1, source_target_pairs={{0,32},{32,64},{64,96},{96,128},{128,160},{160,192},{192,224},{224... | collective-permute-start | bytes 1536008 | tf_op jit(solution)/shard_map/ppermute | solution.py:16
  15.8 62.3 %copy-start = (bf16[1,160,2,160]{1,3,0,2:T(8,128)(2,1)}, bf16[1,160,2,160]{1,3,0,2:T(8,128)(2,1)S(1)}, u32[]{:S(2)}) copy-start(bf16[1,160,2,160]{1,3,0,2:T(8,128)(2,1)S(1)} %get-tuple-element.32) | copy-start | bytes 307204
  15.8 62.3 %copy-start.1 = (bf16[1,160,2,160]{1,3,0,2:T(8,128)(2,1)}, bf16[1,160,2,160]{1,3,0,2:T(8,128)(2,1)S(1)}, u32[]{:S(2)}) copy-start(bf16[1,160,2,160]{1,3,0,2:T(8,128)(2,1)S(1)} %get-tuple-element.33) | copy-start | bytes 307204
  41.0 36.5 %all-to-all-start = ((bf16[1,2,5,160,160]{4,1,2,0,3:T(2,128)(2,1)}), bf16[1,2,5,160,160]{4,1,2,0,3:T(2,128)(2,1)S(1)}, u32[]{:S(2)}, u32[]{:S(2)}) async-start(bf16[1,2,5,160,160]{4,1,2,0,3:T(2,128)(2,1)} %copy.144), calls=%async_computation | async-start | bytes 1638400 | tf_op jit(solution)/shard_map/while/body/eval_jaxpr/all_to_all | solution.py:129
